TPU v7x, 32 devices: a whole 2x2x4 slice. The times are simulated.
32 devices in a mesh: clips: 2 (over x), tm: 4 (over y, core), height: 4 (over z).
Axes of the slice: x: 2, y: 2, z: 4, core: 2. Of those that a mesh axis runs over, the one named last changes fastest.
Arguments:
- features: bfloat16 [16, 16, 96, 512], P(('clips', 'tm'), 'height'), parts along dimension 0, may hold values from -1000 to 1000
- gain: float32 [512], replicated, may hold values from 0.1 to 1.9
- shift: float32 [512], replicated, may hold values from -3 to 3
- kernel: bfloat16 [3, 3, 3, 512, 256], replicated, may hold values from -0.0546875 to 0.0546875
- bias: float32 [256], replicated, may hold values from -3 to 3
Outputs:
- decoded: bfloat16 [16, 16, 96, 256], P(('clips', 'tm'), 'height'), parts along dimension 0
There are 2 independent parts, one for each index of `clips`. A program takes and returns all parts, laid end to end along the dimension named above; an argument that names none is the same for every part. Nothing has to cross between parts.
All inputs are finite; a program needn't handle non-finite values.
Results may differ from a plain program's by a relative error of at most 0.0055.
Values may be sent and summed in bfloat16 or wider, within the bound.
A program may use at most 64 MiB of HBM per device.

v0:
```python
import functools

import jax
import jax.numpy as jnp
from jax import lax
from jax.experimental import pallas as pl
from jax.experimental.pallas import tpu as pltpu
from jax.sharding import PartitionSpec as P

GROUPS = 32
EPSILON = 1e-06
MESH = pl.DeviceIdType.MESH
F32 = jnp.float32
BF16 = jnp.bfloat16


LANES = 128


def group_sums(values, group):
    lanes = values.shape[-1]
    lane = lax.broadcasted_iota(jnp.int32, values.shape, values.ndim - 1)
    step = 1
    while step < group:
        up = pltpu.roll(values, lanes - step, values.ndim - 1)
        down = pltpu.roll(values, step, values.ndim - 1)
        values = values + jnp.where((lane & step) == 0, up, down)
        step *= 2
    return values


def own_lanes(parts):
    lane = lax.broadcasted_iota(jnp.int32, (parts, LANES), 1)
    row = lax.broadcasted_iota(jnp.int32, (parts, LANES), 0)
    return lax.rem(lane, parts) == row


def body(
    n_tm,
    n_h,
    x_hbm,
    gain_hbm,
    shift_hbm,
    w_hbm,
    bias_hbm,
    out_ref,
    x_vm,
    gain_ref,
    shift_ref,
    bias_ref,
    w_vm,
    top_vm,
    bot_vm,
    stats,
    lhs,
    prod,
    nbuf,
    rbuf,
    x_sem,
    p_sem,
    w_sem,
    s_send,
    s_recv,
    h_send,
    h_recv,
    n_send,
    n_recv,
):
    frames, rows, cols, channels = x_vm.shape
    per_group = channels // GROUPS
    tm = lax.axis_index("tm")
    hh = lax.axis_index("height")

    barrier = pltpu.get_barrier_semaphore()
    count = n_tm * n_h
    me = tm * n_h + hh

    def peer(d):
        other = lax.rem(me + d, count)
        return {"tm": lax.div(other, n_h), "height": lax.rem(other, n_h)}

    for d in range(1, count):
        pl.semaphore_signal(barrier, inc=1, device_id=peer(d), device_id_type=MESH)
    x_copies = [pltpu.make_async_copy(x_hbm.at[f], x_vm.at[f], x_sem.at[f]) for f in range(frames)]
    for copy in x_copies:
        copy.start()
    small = ((gain_hbm, gain_ref), (shift_hbm, shift_ref), (bias_hbm, bias_ref))
    p_copies = [pltpu.make_async_copy(*pair, p_sem.at[i]) for i, pair in enumerate(small)]
    for copy in p_copies:
        copy.start()
    w_copies = [
        [pltpu.make_async_copy(w_hbm.at[a, :, c], w_vm.at[a, c], w_sem.at[a, c]) for c in range(3)]
        for a in range(3)
    ]
    sums = jnp.zeros((8, channels), F32)
    squares = jnp.zeros((8, channels), F32)
    for f in range(frames):
        x_copies[f].wait()
        for r in range(rows):
            v = x_vm[f, r].astype(F32).reshape(cols // 8, 8, channels)
            sums = sums + jnp.sum(v, axis=0)
            squares = squares + jnp.sum(v * v, axis=0)
    blocks = channels // LANES
    parts = 2 * blocks
    assert parts <= per_group <= LANES
    sums = jnp.sum(sums, axis=0, keepdims=True)
    squares = jnp.sum(squares, axis=0, keepdims=True)
    stacked = jnp.concatenate(
        [v[:, k * LANES : (k + 1) * LANES] for v in (sums, squares) for k in range(blocks)], axis=0
    )
    spread = jnp.where(own_lanes(parts), group_sums(stacked, per_group), 0.0)
    stats[0] = jnp.sum(spread, axis=0, keepdims=True)

    pl.semaphore_wait(barrier, count - 1)

    shares = [
        pltpu.make_async_remote_copy(
            src_ref=stats.at[0],
            dst_ref=stats.at[d],
            send_sem=s_send.at[d],
            recv_sem=s_recv.at[d],
            device_id=peer(d),
            device_id_type=MESH,
        )
        for d in range(1, count)
    ]
    for copy in shares:
        copy.start()
    for a in range(3):
        for c in range(3):
            w_copies[a][c].start()
    to_next = pltpu.make_async_remote_copy(
        src_ref=x_hbm.at[:, rows - 1],
        dst_ref=top_vm,
        send_sem=h_send.at[0],
        recv_sem=h_recv.at[0],
        device_id={"height": lax.rem(hh + 1, n_h)},
        device_id_type=MESH,
    )
    to_last = pltpu.make_async_remote_copy(
        src_ref=x_hbm.at[:, 0],
        dst_ref=bot_vm,
        send_sem=h_send.at[1],
        recv_sem=h_recv.at[1],
        device_id={"height": lax.rem(hh + n_h - 1, n_h)},
        device_id_type=MESH,
    )
    @pl.when(hh < n_h - 1)
    def _():
        to_next.start()

    @pl.when(hh > 0)
    def _():
        to_last.start()

    for copy in shares:
        copy.wait_recv()
    total = jnp.sum(stats[...], axis=0)
    for copy in p_copies:
        copy.wait()
    cells = n_tm * n_h * frames * rows * cols * per_group
    means = group_sums(jnp.where(own_lanes(parts), total, 0.0), parts) * (1.0 / cells)
    mean = means[:blocks]
    var = jnp.maximum(means[blocks:] - mean * mean, 0.0)
    inverse = lax.rsqrt(var + EPSILON)

    def one_row(v):
        return jnp.concatenate([v[k : k + 1] for k in range(blocks)], axis=1)

    half_scale = 0.5 * gain_ref[...] * one_row(inverse)
    half_offset = 0.5 * shift_ref[...] - one_row(mean) * half_scale

    def activate(v):
        h = v.astype(F32) * half_scale + half_offset
        return (h + h * jnp.tanh(h)).astype(BF16)

    row_sets = (tuple(range(1, rows - 1)), (0, rows - 1))
    per_set = 2 * cols

    def place(row, f, value):
        for s in range(2):
            for q, i in enumerate(row_sets[s]):
                b = row - i + 1
                if 0 <= b <= 2:
                    lhs[
                        s,
                        f * per_set + q * cols : f * per_set + (q + 1) * cols,
                        b * channels : (b + 1) * channels,
                    ] = value

    for f in range(frames):
        for r in range(rows):
            place(r, f, activate(x_vm[f, r]))

    m = frames * per_set
    position = lax.rem(lax.broadcasted_iota(jnp.int32, (m, 1), 0), cols)
    not_first = position != 0
    not_last = position != cols - 1

    def product(a, s):
        def tap(c, start, stop):
            weights = w_vm[a, c].reshape(3 * channels, w_vm.shape[-1])
            return jnp.dot(lhs[s, start:stop], weights, preferred_element_type=F32)

        low = jnp.where(not_first, pltpu.roll(tap(0, 0, m), 1, 0), 0.0)
        high = jnp.where(not_last, pltpu.roll(tap(2, 0, m), m - 1, 0), 0.0)
        sides = low + high
        for start in (0, per_set):
            stop = start + per_set
            prod[a, s, start:stop] = sides[start:stop] + tap(1, start, stop)

    def sends(s, k):
        return pltpu.make_async_remote_copy(
            src_ref=nbuf.at[s, k],
            dst_ref=rbuf.at[s, k],
            send_sem=n_send.at[s, k],
            recv_sem=n_recv.at[s, k],
            device_id={"tm": lax.rem(tm + 1, n_tm)},
            device_id_type=MESH,
        )

    def send(s, k):
        @pl.when(tm < n_tm - 1)
        def _():
            sends(s, k).start()

    def wait_weights(a):
        for c in range(3):
            w_copies[a][c].wait()

    def early(s):
        if s == 0:
            wait_weights(0)
            wait_weights(1)
        product(0, s)
        nbuf[s, 1] = prod[0, s, per_set:].astype(BF16)
        send(s, 1)
        product(1, s)
        nbuf[s, 0] = (prod[0, s, :per_set] + prod[1, s, per_set:]).astype(BF16)
        send(s, 0)

    early(0)

    @pl.when(hh > 0)
    def _():
        to_next.wait_recv()
        for f in range(frames):
            place(-1, f, activate(top_vm[f]))

    @pl.when(hh == 0)
    def _():
        for f in range(frames):
            place(-1, f, jnp.zeros((cols, channels), BF16))

    @pl.when(hh < n_h - 1)
    def _():
        to_last.wait_recv()
        for f in range(frames):
            place(rows, f, activate(bot_vm[f]))

    @pl.when(hh == n_h - 1)
    def _():
        for f in range(frames):
            place(rows, f, jnp.zeros((cols, channels), BF16))

    wait_weights(2)
    early(1)
    product(2, 0)
    product(2, 1)

    bias = bias_ref[...]
    for s in range(2):
        for k in (1, 0):

            @pl.when(tm > 0)
            def _():
                sends(s, k).wait_recv()

            own = prod[2, s, k * per_set : (k + 1) * per_set]
            first = prod[0, s, :per_set]
            other = prod[1, s, :per_set]
            if k == 1:
                own = own + other
            else:
                first = first + other
            earlier = jnp.where(tm == 0, first, rbuf[s, k].astype(F32))
            value = (own + earlier + bias).astype(BF16)
            for q, i in enumerate(row_sets[s]):
                out_ref[k, i] = value[q * cols : (q + 1) * cols]

    for copy in shares:
        copy.wait_send()

    @pl.when(hh < n_h - 1)
    def _():
        to_next.wait_send()

    @pl.when(hh > 0)
    def _():
        to_last.wait_send()

    @pl.when(tm < n_tm - 1)
    def _():
        for s in range(2):
            for k in range(2):
                sends(s, k).wait_send()


def solution(mesh):
    n_tm, n_h = mesh.shape["tm"], mesh.shape["height"]

    def on_device(features, gain, shift, kernel, bias):
        frames, rows, cols, channels = features.shape
        c_out = kernel.shape[-1]
        assert frames == 2 and rows == 4
        per_set = 2 * cols
        vmem = pl.BlockSpec(memory_space=pltpu.VMEM)
        hbm = pl.BlockSpec(memory_space=pltpu.HBM)
        dma = pltpu.SemaphoreType.DMA
        return pl.pallas_call(
            functools.partial(body, n_tm, n_h),
            out_shape=pltpu.VMEM((frames, rows, cols, c_out), BF16),
            in_specs=[hbm] * 5,
            out_specs=vmem,
            scratch_shapes=[
                pltpu.VMEM((frames, rows, cols, channels), BF16),
                pltpu.VMEM((1, channels), F32),
                pltpu.VMEM((1, channels), F32),
                pltpu.VMEM((1, c_out), F32),
                pltpu.VMEM((3, 3, 3, channels, c_out), BF16),
                pltpu.VMEM((frames, cols, channels), BF16),
                pltpu.VMEM((frames, cols, channels), BF16),
                pltpu.VMEM((n_tm * n_h, 1, LANES), F32),
                pltpu.VMEM((2, frames * per_set, 3 * channels), BF16),
                pltpu.VMEM((3, 2, frames * per_set, c_out), F32),
                pltpu.VMEM((2, 2, per_set, c_out), BF16),
                pltpu.VMEM((2, 2, per_set, c_out), BF16),
                dma((frames,)),
                dma((3,)),
                dma((3, 3)),
                dma((n_tm * n_h,)),
                dma((n_tm * n_h,)),
                dma((2,)),
                dma((2,)),
                dma((2, 2)),
                dma((2, 2)),
            ],
            compiler_params=pltpu.CompilerParams(
                collective_id=0, has_side_effects=True, vmem_limit_bytes=67_043_328 - 640 * 2**10
            ),
        )(features, gain.reshape(1, -1), shift.reshape(1, -1), kernel, bias.reshape(1, -1))

    placed = (P(("clips", "tm"), "height", None, None), P(), P(), P(), P())
    return jax.shard_map(
        on_device,
        mesh=mesh,
        in_specs=placed,
        out_specs=P(("clips", "tm"), "height", None, None),
        check_vma=False,
    )
```

profile of v0, /device:TPU:0, one launch (start us, length us, event | category | flops | bytes accessed | tf_op | source)
XLA Modules:
  0.0 17.8 jit_solution(11448937439403478918)
XLA Ops:
  0.0 17.1 %shard_map.55 = bf16[2,4,96,256]{3,2,1,0:T(8,128)(2,1)S(1)} custom-call(bf16[2,4,96,512]{3,2,1,0:T(8,128)(2,1)} %x_hbm.1, f32[1,512]{1,0:T(1,128)} %bitcast.3, f32[1,512]{1,0:T(1,128)} %bitcast.4, bf16[3,3,3,512,256]{4,3,2,1,0:T(8,128)(2,1)} %w_hbm.1, f32[1,256]{1,0:T(1,128)} %bitcast.5), custom_call_target="tpu_custom_call" | custom-call | tf_op jit(solution)/shard_map/pallas_call | solution.py:320
  17.1 0.7 %copy.7 = bf16[2,4,96,256]{3,2,1,0:T(8,128)(2,1)} copy(bf16[2,4,96,256]{3,2,1,0:T(8,128)(2,1)S(1)} %shard_map.55) | data formatting | bytes 786432
where the time goes:
time: 18 us; the launch traced here: 17.8 us
  Pallas kernels  17.1 us (95%)
  local copies, waits for them, and re-layouts  0.75 us (4%)
    pallas_call x1, Pallas kernels, on_device(): pl.pallas_call(functools.partial(body, n_tm, n_h), out_shape=pltpu.VMEM((...  17.1 us
    unnamed x1, local copies, waits for them, and re-layouts  0.75 us

commit v1 on v0

v1 whole, which is shorter than its diff:
```python
import functools

import jax
import jax.numpy as jnp
from jax import lax
from jax.experimental import pallas as pl
from jax.experimental.pallas import tpu as pltpu
from jax.sharding import PartitionSpec as P

GROUPS = 32
EPSILON = 1e-06
MESH = pl.DeviceIdType.MESH
F32 = jnp.float32
BF16 = jnp.bfloat16


LANES = 128


def group_sums(values, group):
    lanes = values.shape[-1]
    lane = lax.broadcasted_iota(jnp.int32, values.shape, values.ndim - 1)
    step = 1
    while step < group:
        up = pltpu.roll(values, lanes - step, values.ndim - 1)
        down = pltpu.roll(values, step, values.ndim - 1)
        values = values + jnp.where((lane & step) == 0, up, down)
        step *= 2
    return values


def own_lanes(parts):
    lane = lax.broadcasted_iota(jnp.int32, (parts, LANES), 1)
    row = lax.broadcasted_iota(jnp.int32, (parts, LANES), 0)
    return lax.rem(lane, parts) == row


def body(
    n_tm,
    n_h,
    x_hbm,
    gain_hbm,
    shift_hbm,
    w_hbm,
    bias_hbm,
    out_ref,
    x_vm,
    small,
    w_vm,
    u_vm,
    top_vm,
    bot_vm,
    stats,
    lhs,
    prod,
    nbuf,
    rbuf,
    x_sem,
    p_sem,
    w_sem,
    s_send,
    s_recv,
    h_send,
    h_recv,
    n_send,
    n_recv,
):
    frames, rows, cols, channels = x_vm.shape
    c_out = w_vm.shape[-1]
    per_group = channels // GROUPS
    tm = lax.axis_index("tm")
    hh = lax.axis_index("height")

    barrier = pltpu.get_barrier_semaphore()
    count = n_tm * n_h
    me = tm * n_h + hh

    def peer(d):
        other = lax.rem(me + d, count)
        return {"tm": lax.div(other, n_h), "height": lax.rem(other, n_h)}

    for d in range(1, count):
        pl.semaphore_signal(barrier, inc=1, device_id=peer(d), device_id_type=MESH)
    half = rows // 2
    x_copies = [
        pltpu.make_async_copy(
            x_hbm.at[f, q * half : (q + 1) * half], x_vm.at[f, q * half : (q + 1) * half], x_sem.at[f, q]
        )
        for f in range(frames)
        for q in range(2)
    ]
    for copy in x_copies:
        copy.start()
    ends = (0, channels, 2 * channels, 2 * channels + c_out)
    for i, ref in enumerate((gain_hbm, shift_hbm, bias_hbm)):
        pltpu.make_async_copy(ref, small.at[:, ends[i] : ends[i + 1]], p_sem).start()
    w_copies = [
        pltpu.make_async_copy(w_hbm.at[:, :, c], w_vm.at[:, c], w_sem.at[c]) for c in range(3)
    ]
    with jax.named_scope("a_sums"):
        sums = jnp.zeros((8, channels), F32)
        squares = jnp.zeros((8, channels), F32)
        for p in range(2 * frames):
            with jax.named_scope("x_wait"):
                x_copies[p].wait()
            if p == 2 * frames - 1:
                for copy in w_copies:
                    copy.start()
            f = p // 2
            for r in range(p % 2 * half, p % 2 * half + half):
                v = x_vm[f, r].astype(F32).reshape(cols // 8, 8, channels)
                sums = sums + jnp.sum(v, axis=0)
                squares = squares + jnp.sum(v * v, axis=0)
    with jax.named_scope("b_stat"):
        blocks = channels // LANES
        parts = 2 * blocks
        assert parts <= per_group <= LANES
        sums = jnp.sum(sums, axis=0, keepdims=True)
        squares = jnp.sum(squares, axis=0, keepdims=True)
        stacked = jnp.concatenate(
            [v[:, k * LANES : (k + 1) * LANES] for v in (sums, squares) for k in range(blocks)], axis=0
        )
        spread = jnp.where(own_lanes(parts), group_sums(stacked, per_group), 0.0)
        stats[0] = jnp.sum(spread, axis=0, keepdims=True)

    with jax.named_scope("c_barrier"):
        pl.semaphore_wait(barrier, count - 1)

    shares = [
        pltpu.make_async_remote_copy(
            src_ref=stats.at[0],
            dst_ref=stats.at[d],
            send_sem=s_send,
            recv_sem=s_recv,
            device_id=peer(d),
            device_id_type=MESH,
        )
        for d in range(1, count)
    ]
    for copy in shares:
        copy.start()
    to_next = pltpu.make_async_remote_copy(
        src_ref=x_vm.at[:, rows - 1],
        dst_ref=top_vm,
        send_sem=h_send.at[0],
        recv_sem=h_recv.at[0],
        device_id={"height": lax.rem(hh + 1, n_h)},
        device_id_type=MESH,
    )
    to_last = pltpu.make_async_remote_copy(
        src_ref=x_vm.at[:, 0],
        dst_ref=bot_vm,
        send_sem=h_send.at[1],
        recv_sem=h_recv.at[1],
        device_id={"height": lax.rem(hh + n_h - 1, n_h)},
        device_id_type=MESH,
    )

    @pl.when(hh < n_h - 1)
    def _():
        to_next.start()

    @pl.when(hh > 0)
    def _():
        to_last.start()

    step = 64
    for c in range(3):
        with jax.named_scope("w_wait"):
            w_copies[c].wait()

        with jax.named_scope("w_trans"):
            for b in range(3):

                @pl.loop(0, channels // step)
                def _(i):
                    part = pl.ds(pl.multiple_of(i * step, step), step)
                    g0, g1, g2 = (w_vm[a, c, b, part].astype(F32) for a in range(3))
                    even = 0.5 * (g0 + g2)
                    odd = 0.5 * g1
                    u_vm[0, c, b, part] = (even + odd).astype(BF16)
                    u_vm[1, c, b, part] = (even - odd).astype(BF16)

    pltpu.make_async_copy(small, small, p_sem).wait()
    with jax.named_scope("e_shares"):
        pltpu.make_async_copy(stats.at[1:], stats.at[1:], s_recv).wait()
    total = jnp.sum(stats[...], axis=0)
    cells = n_tm * n_h * frames * rows * cols * per_group
    means = group_sums(jnp.where(own_lanes(parts), total, 0.0), parts) * (1.0 / cells)
    mean = means[:blocks]
    var = jnp.maximum(means[blocks:] - mean * mean, 0.0)
    inverse = lax.rsqrt(var + EPSILON)

    def one_row(v):
        return jnp.concatenate([v[k : k + 1] for k in range(blocks)], axis=1)

    half_scale = 0.5 * small[:, ends[0] : ends[1]] * one_row(inverse)
    half_offset = 0.5 * small[:, ends[1] : ends[2]] - one_row(mean) * half_scale

    def activate(v):
        h = v.astype(F32) * half_scale + half_offset
        return (h + h * jnp.tanh(h)).astype(BF16)

    first = jnp.where(tm == 0, 1.0, 0.0).astype(F32)
    at = [(u - first).astype(BF16) for u in (0.0, 1.0, -1.0)]

    def place(row, v0, v1):
        f0, f1 = activate(v0), activate(v1)
        for u in range(3):
            lhs[u, row + 1] = f0 + at[u] * f1
        lhs[3, row + 1] = f1

    with jax.named_scope("f_act"):
        for r in range(rows):
            place(r, x_vm[0, r], x_vm[1, r])

    m = 2 * cols
    position = lax.rem(lax.broadcasted_iota(jnp.int32, (m, 1), 0), cols)
    not_first = position != 0
    not_last = position != cols - 1
    row_sets = (tuple(range(1, rows - 1)), (0, rows - 1))

    def weights(u, c):
        ref = (w_vm.at[2], u_vm.at[0], u_vm.at[1], w_vm.at[0])[u]
        return ref[c].reshape(3 * channels, c_out)

    def product(u, s):
        def tap(c, depth=slice(None), r=slice(None)):
            rows_of = [
                jnp.concatenate([lhs[u, i + b] for i in row_sets[s][r]], axis=0) for b in range(3)
            ]
            return jnp.dot(
                jnp.concatenate(rows_of, axis=1)[:, depth],
                weights(u, c)[depth],
                preferred_element_type=F32,
            )

        def low_of(v):
            return jnp.where(not_first, pltpu.roll(v, 1, 0), 0.0)

        high = jnp.where(not_last, pltpu.roll(tap(2), m - 1, 0), 0.0)
        cut = 3 * channels // 2
        if u in (2, 3):
            low = low_of(tap(0, slice(0, cut))) + low_of(tap(0, slice(cut, None)))
        else:
            low = low_of(tap(0))
        prod[u, s] = low + high + tap(1)

    def sends(s, k):
        return pltpu.make_async_remote_copy(
            src_ref=nbuf.at[s, k],
            dst_ref=rbuf.at[s, k],
            send_sem=n_send,
            recv_sem=n_recv.at[s],
            device_id={"tm": lax.rem(tm + 1, n_tm)},
            device_id_type=MESH,
        )

    def send(s, k):
        @pl.when(tm < n_tm - 1)
        def _():
            sends(s, k).start()

    def early(s):
        product(3, s)
        nbuf[s, 1] = prod[3, s].astype(BF16)
        send(s, 1)
        product(0, s)
        product(1, s)
        product(2, s)
        later = prod[1, s] + prod[2, s] - prod[0, s] + first * prod[3, s]
        nbuf[s, 0] = later.astype(BF16)
        send(s, 0)

    with jax.named_scope("g_early0"):
        early(0)

    with jax.named_scope("h_halo"):
        @pl.when(hh > 0)
        def _():
            to_next.wait_recv()
            place(-1, top_vm[0], top_vm[1])

        @pl.when(hh == 0)
        def _():
            for u in range(4):
                lhs[u, 0] = jnp.zeros((cols, channels), BF16)

        @pl.when(hh < n_h - 1)
        def _():
            to_last.wait_recv()
            place(rows, bot_vm[0], bot_vm[1])

        @pl.when(hh == n_h - 1)
        def _():
            for u in range(4):
                lhs[u, rows + 1] = jnp.zeros((cols, channels), BF16)

    with jax.named_scope("i_early1"):
        early(1)

    bias = small[:, ends[2] : ends[3]]
    with jax.named_scope("k_out"):
        for s in range(2):

            @pl.when(tm > 0)
            def _():
                pltpu.make_async_copy(rbuf.at[s], rbuf.at[s], n_recv.at[s]).wait()

            for k in (1, 0):
                at_0, at_1, at_minus, at_inf = (prod[u, s] for u in range(4))
                if k == 1:
                    own = jnp.where(tm == 0, 2.0 * at_1 - at_0, at_1 - at_minus - at_inf)
                else:
                    own = jnp.where(tm == 0, 2.0 * at_1, at_0)
                earlier = jnp.where(tm == 0, 0.0, rbuf[s, k].astype(F32))
                value = (own + earlier + bias).astype(BF16)
                for q, i in enumerate(row_sets[s]):
                    out_ref[k, i] = value[q * cols : (q + 1) * cols]

    with jax.named_scope("l_tail"):
        pltpu.make_async_copy(stats.at[1:], stats.at[1:], s_send).wait()

        @pl.when(hh < n_h - 1)
        def _():
            to_next.wait_send()

        @pl.when(hh > 0)
        def _():
            to_last.wait_send()

        @pl.when(tm < n_tm - 1)
        def _():
            pltpu.make_async_copy(nbuf, nbuf, n_send).wait()


def solution(mesh):
    n_tm, n_h = mesh.shape["tm"], mesh.shape["height"]

    def on_device(features, gain, shift, kernel, bias):
        frames, rows, cols, channels = features.shape
        c_out = kernel.shape[-1]
        assert frames == 2 and rows == 4
        per_set = 2 * cols
        vmem = pl.BlockSpec(memory_space=pltpu.VMEM)
        hbm = pl.BlockSpec(memory_space=pltpu.HBM)
        dma = pltpu.SemaphoreType.DMA
        return pl.pallas_call(
            functools.partial(body, n_tm, n_h),
            out_shape=pltpu.VMEM((frames, rows, cols, c_out), BF16),
            in_specs=[hbm] * 5,
            out_specs=vmem,
            scratch_shapes=[
                pltpu.VMEM((frames, rows, cols, channels), BF16),
                pltpu.VMEM((1, 2 * channels + c_out), F32),
                pltpu.VMEM((3, 3, 3, channels, c_out), BF16),
                pltpu.VMEM((2, 3, 3, channels, c_out), BF16),
                pltpu.VMEM((frames, cols, channels), BF16),
                pltpu.VMEM((frames, cols, channels), BF16),
                pltpu.VMEM((n_tm * n_h, 1, LANES), F32),
                pltpu.VMEM((4, rows + 2, cols, channels), BF16),
                pltpu.VMEM((4, 2, per_set, c_out), F32),
                pltpu.VMEM((2, 2, per_set, c_out), BF16),
                pltpu.VMEM((2, 2, per_set, c_out), BF16),
                dma((frames, 2)),
                dma,
                dma((3,)),
                dma,
                dma,
                dma((2,)),
                dma((2,)),
                dma,
                dma((2,)),
            ],
            compiler_params=pltpu.CompilerParams(
                collective_id=0, has_side_effects=True, vmem_limit_bytes=67_043_328 - 640 * 2**10
            ),
        )(features, gain.reshape(1, -1), shift.reshape(1, -1), kernel, bias.reshape(1, -1))

    placed = (P(("clips", "tm"), "height", None, None), P(), P(), P(), P())
    return jax.shard_map(
        on_device,
        mesh=mesh,
        in_specs=placed,
        out_specs=P(("clips", "tm"), "height", None, None),
        check_vma=False,
    )
```

time: 18 us -> 16.4 us (0.911)
  Pallas kernels: 17.1 us -> 15.5 us
    pallas_call x1, Pallas kernels: 17.1 us -> 15.5 us  [on_device(): pl.pallas_call(functools.partial(body, n_tm, n_h), out_shape=pltpu.VMEM((...]
where the time goes in v1:
time: 16.4 us; the launch traced here: 16.2 us
  Pallas kernels  15.5 us (95%)
  local copies, waits for them, and re-layouts  0.75 us (5%)
    pallas_call x1, Pallas kernels, on_device(): pl.pallas_call(functools.partial(body, n_tm, n_h), out_shape=pltpu.VMEM((...  15.5 us
    unnamed x1, local copies, waits for them, and re-layouts  0.75 us

profile of v1, /device:TPU:0, one launch (start us, length us, event | category | flops | bytes accessed | tf_op | source)
XLA Modules:
  0.0 16.2 jit_solution(14777118163220758815)
XLA Ops:
  0.0 15.5 %shard_map.55 = bf16[2,4,96,256]{3,2,1,0:T(8,128)(2,1)S(1)} custom-call(bf16[2,4,96,512]{3,2,1,0:T(8,128)(2,1)} %x_hbm.1, f32[1,512]{1,0:T(1,128)} %bitcast.3, f32[1,512]{1,0:T(1,128)} %bitcast.4, bf16[3,3,3,512,256]{4,3,2,1,0:T(8,128)(2,1)} %w_hbm.1, f32[1,256]{1,0:T(1,128)} %bitcast.5), custom_call_target="tpu_custom_call" | custom-call | tf_op jit(solution)/shard_map/pallas_call | solution.py:348
  15.5 0.7 %copy.7 = bf16[2,4,96,256]{3,2,1,0:T(8,128)(2,1)} copy(bf16[2,4,96,256]{3,2,1,0:T(8,128)(2,1)S(1)} %shard_map.55) | data formatting | bytes 786432

commit v2 on v1

--- a/solution.py
+++ b/solution.py
@@ -18,15 +18,15 @@
 
 
 def group_sums(values, group):
-    lanes = values.shape[-1]
-    lane = lax.broadcasted_iota(jnp.int32, values.shape, values.ndim - 1)
-    step = 1
-    while step < group:
-        up = pltpu.roll(values, lanes - step, values.ndim - 1)
-        down = pltpu.roll(values, step, values.ndim - 1)
-        values = values + jnp.where((lane & step) == 0, up, down)
-        step *= 2
-    return values
+    lane = lax.rem(lax.broadcasted_iota(jnp.int32, values.shape, 1), group)
+    terms = [values]
+    for j in range(1, group):
+        up = pltpu.roll(values, LANES - j, 1)
+        down = pltpu.roll(values, group - j, 1)
+        terms.append(jnp.where(lane < group - j, up, down))
+    while len(terms) > 1:
+        terms = [sum(terms[i : i + 2][1:], terms[i]) for i in range(0, len(terms), 2)]
+    return terms[0]
 
 
 def own_lanes(parts):
@@ -53,6 +53,7 @@
     stats,
     lhs,
     prod,
+    own,
     nbuf,
     rbuf,
     x_sem,
@@ -79,8 +80,6 @@
         other = lax.rem(me + d, count)
         return {"tm": lax.div(other, n_h), "height": lax.rem(other, n_h)}
 
-    for d in range(1, count):
-        pl.semaphore_signal(barrier, inc=1, device_id=peer(d), device_id_type=MESH)
     half = rows // 2
     x_copies = [
         pltpu.make_async_copy(
@@ -91,6 +90,8 @@
     ]
     for copy in x_copies:
         copy.start()
+    for d in range(1, count):
+        pl.semaphore_signal(barrier, inc=1, device_id=peer(d), device_id_type=MESH)
     ends = (0, channels, 2 * channels, 2 * channels + c_out)
     for i, ref in enumerate((gain_hbm, shift_hbm, bias_hbm)):
         pltpu.make_async_copy(ref, small.at[:, ends[i] : ends[i + 1]], p_sem).start()
@@ -137,32 +138,29 @@
         )
         for d in range(1, count)
     ]
-    for copy in shares:
-        copy.start()
-    to_next = pltpu.make_async_remote_copy(
-        src_ref=x_vm.at[:, rows - 1],
-        dst_ref=top_vm,
-        send_sem=h_send.at[0],
-        recv_sem=h_recv.at[0],
-        device_id={"height": lax.rem(hh + 1, n_h)},
-        device_id_type=MESH,
-    )
-    to_last = pltpu.make_async_remote_copy(
-        src_ref=x_vm.at[:, 0],
-        dst_ref=bot_vm,
-        send_sem=h_send.at[1],
-        recv_sem=h_recv.at[1],
-        device_id={"height": lax.rem(hh + n_h - 1, n_h)},
-        device_id_type=MESH,
-    )
-
-    @pl.when(hh < n_h - 1)
-    def _():
-        to_next.start()
-
-    @pl.when(hh > 0)
-    def _():
-        to_last.start()
+    for dh in (*range(1, n_h), 0):
+        for dt in range(n_tm):
+            if (dt, dh) != (0, 0):
+                shares[dt * n_h + dh - 1].start()
+    edges = ((rows - 1, top_vm, 1, hh < n_h - 1), (0, bot_vm, n_h - 1, hh > 0))
+
+    def halo(e, f):
+        row, ref, up, _ = edges[e]
+        return pltpu.make_async_remote_copy(
+            src_ref=x_vm.at[f, row],
+            dst_ref=ref.at[f],
+            send_sem=h_send.at[e],
+            recv_sem=h_recv.at[e, f],
+            device_id={"height": lax.rem(hh + up, n_h)},
+            device_id_type=MESH,
+        )
+
+    for e in range(2):
+
+        @pl.when(edges[e][3])
+        def _():
+            for f in (1, 0):
+                halo(e, f).start()
 
     step = 64
     for c in range(3):
@@ -180,6 +178,7 @@
                     odd = 0.5 * g1
                     u_vm[0, c, b, part] = (even + odd).astype(BF16)
                     u_vm[1, c, b, part] = (even - odd).astype(BF16)
+                    u_vm[2, c, b, part] = (g1 + g2).astype(BF16)
 
     pltpu.make_async_copy(small, small, p_sem).wait()
     with jax.named_scope("e_shares"):
@@ -201,18 +200,29 @@
         h = v.astype(F32) * half_scale + half_offset
         return (h + h * jnp.tanh(h)).astype(BF16)
 
-    first = jnp.where(tm == 0, 1.0, 0.0).astype(F32)
-    at = [(u - first).astype(BF16) for u in (0.0, 1.0, -1.0)]
-
-    def place(row, v0, v1):
-        f0, f1 = activate(v0), activate(v1)
-        for u in range(3):
-            lhs[u, row + 1] = f0 + at[u] * f1
-        lhs[3, row + 1] = f1
+    is_first = jnp.where(tm == 0, 1, 0)
+    first = is_first.astype(F32)
+    F_0, F_1, LESS, PLUS, LESS_TWICE = range(5)
+    at_0, at_1, at_minus = 2 * is_first, 3 - 3 * is_first, 2 + 2 * is_first
+
+    def place_first(row, f0):
+        f1 = lhs[F_1, row + 1]
+        for u, value in ((F_0, f0), (LESS, f0 - f1), (PLUS, f0 + f1)):
+            lhs[u, row + 1] = value
 
     with jax.named_scope("f_act"):
         for r in range(rows):
-            place(r, x_vm[0, r], x_vm[1, r])
+            lhs[F_1, r + 1] = activate(x_vm[1, r])
+        for r in range(rows):
+            place_first(r, activate(x_vm[0, r]))
+
+    def edge(e, f):
+        @pl.when(edges[1 - e][3])
+        def _():
+            halo(e, f).wait_recv()
+
+        value = activate(edges[e][1][f])
+        return jnp.where(edges[1 - e][3], value, jnp.zeros_like(value))
 
     m = 2 * cols
     position = lax.rem(lax.broadcasted_iota(jnp.int32, (m, 1), 0), cols)
@@ -220,31 +230,34 @@
     not_last = position != cols - 1
     row_sets = (tuple(range(1, rows - 1)), (0, rows - 1))
 
-    def weights(u, c):
-        ref = (w_vm.at[2], u_vm.at[0], u_vm.at[1], w_vm.at[0])[u]
-        return ref[c].reshape(3 * channels, c_out)
-
-    def product(u, s):
-        def tap(c, depth=slice(None), r=slice(None)):
+    cut = 3 * channels // 2
+
+    def low_of(v):
+        return jnp.where(not_first, pltpu.roll(v, 1, 0), 0.0)
+
+    def high_of(v):
+        return jnp.where(not_last, pltpu.roll(v, m - 1, 0), 0.0)
+
+    def taps(u, weights, s, split=False):
+        def tap(c, depth=slice(None)):
             rows_of = [
-                jnp.concatenate([lhs[u, i + b] for i in row_sets[s][r]], axis=0) for b in range(3)
+                jnp.concatenate([lhs[u, i + b] for i in row_sets[s]], axis=0) for b in range(3)
             ]
             return jnp.dot(
                 jnp.concatenate(rows_of, axis=1)[:, depth],
-                weights(u, c)[depth],
+                weights[c].reshape(3 * channels, c_out)[depth],
                 preferred_element_type=F32,
             )
 
-        def low_of(v):
-            return jnp.where(not_first, pltpu.roll(v, 1, 0), 0.0)
-
-        high = jnp.where(not_last, pltpu.roll(tap(2), m - 1, 0), 0.0)
-        cut = 3 * channels // 2
-        if u in (2, 3):
-            low = low_of(tap(0, slice(0, cut))) + low_of(tap(0, slice(cut, None)))
-        else:
-            low = low_of(tap(0))
-        prod[u, s] = low + high + tap(1)
+        halves = (slice(0, cut), slice(cut, None)) if split else (slice(None),)
+        return tap(1), tap(2), *(tap(0, depth) for depth in halves)
+
+    def merge(parts_of):
+        mid, high, *low = parts_of
+        value = mid + high_of(high)
+        for v in low:
+            value = value + low_of(v)
+        return value
 
     def sends(s, k):
         return pltpu.make_async_remote_copy(
@@ -261,73 +274,84 @@
         def _():
             sends(s, k).start()
 
-    def early(s):
-        product(3, s)
-        nbuf[s, 1] = prod[3, s].astype(BF16)
-        send(s, 1)
-        product(0, s)
-        product(1, s)
-        product(2, s)
-        later = prod[1, s] + prod[2, s] - prod[0, s] + first * prod[3, s]
-        nbuf[s, 0] = later.astype(BF16)
-        send(s, 0)
-
-    with jax.named_scope("g_early0"):
-        early(0)
-
-    with jax.named_scope("h_halo"):
-        @pl.when(hh > 0)
+    bias = small[:, ends[2] : ends[3]]
+
+    def finish(s, k, value):
+        value = value + bias
+        own[s, k] = value
+        put(s, k, value)
+
+    def put(s, k, value):
+        value = value.astype(BF16)
+        for q, i in enumerate(row_sets[s]):
+            out_ref[k, i] = value[q * cols : (q + 1) * cols]
+
+    w_0, w_1, w_2 = (w_vm.at[a] for a in range(3))
+    w_half, w_half_minus, w_sum = (u_vm.at[u] for u in range(3))
+
+    with jax.named_scope("g_inf0"):
+        p_inf = merge(taps(F_1, w_0, 0, split=False))
+        prod[0] = p_inf
+        nbuf[0, 1] = p_inf.astype(BF16)
+        ahead = taps(at_0, w_2, 0)
+        send(0, 1)
+        prod[1] = merge(ahead)
+
+    with jax.named_scope("h_halo1"):
+        for e, row in ((0, -1), (1, rows)):
+            lhs[F_1, row + 1] = edge(e, 1)
+
+    with jax.named_scope("i_inf1"):
+        nbuf[1, 1] = merge(taps(F_1, w_0, 1, split=False)).astype(BF16)
+        for r in range(rows):
+            lhs[LESS_TWICE, r + 1] = lhs[LESS, r + 1] - lhs[F_1, r + 1]
+        ahead = taps(at_1, w_half, 0)
+        send(1, 1)
+        prod[2] = merge(ahead)
+
+    with jax.named_scope("i_rest0"):
+        prod[3] = merge(taps(at_minus, w_half_minus, 0))
+        p_inf, p_0, p_1, p_minus = (prod[i] for i in range(4))
+        nbuf[0, 0] = (p_1 + p_minus - p_0 + first * p_inf).astype(BF16)
+        finish(0, 0, jnp.where(tm == 0, 2.0 * p_1, p_0))
+        finish(0, 1, jnp.where(tm == 0, 2.0 * p_1 - p_0, p_1 - p_minus - p_inf))
+        ahead = taps(F_1, w_1, 1)
+        send(0, 0)
+        prod[1] = merge(ahead)
+
+    with jax.named_scope("h_halo0"):
+        for e, row in ((0, -1), (1, rows)):
+            place_first(row, edge(e, 0))
+
+    with jax.named_scope("j_later1"):
+        prod[0] = merge(taps(F_0, w_0, 1, split=False))
+        nbuf[1, 0] = (prod[0] + prod[1]).astype(BF16)
+        ahead = taps(at_0, w_2, 1)
+        send(1, 0)
+        prod[2] = merge(ahead)
+
+    with jax.named_scope("j_rest1"):
+        prod[3] = merge(taps(at_1, w_sum, 1, split=True))
+        q_2, q_3, q_4, q_5 = (prod[i] for i in range(4))
+        finish(1, 0, jnp.where(tm == 0, q_2 + q_5, q_4))
+        finish(1, 1, q_5 - q_4 + jnp.where(tm == 0, q_2, -q_3))
+
+    with jax.named_scope("k_out"):
+        @pl.when(tm > 0)
         def _():
-            to_next.wait_recv()
-            place(-1, top_vm[0], top_vm[1])
-
-        @pl.when(hh == 0)
-        def _():
-            for u in range(4):
-                lhs[u, 0] = jnp.zeros((cols, channels), BF16)
-
-        @pl.when(hh < n_h - 1)
-        def _():
-            to_last.wait_recv()
-            place(rows, bot_vm[0], bot_vm[1])
-
-        @pl.when(hh == n_h - 1)
-        def _():
-            for u in range(4):
-                lhs[u, rows + 1] = jnp.zeros((cols, channels), BF16)
-
-    with jax.named_scope("i_early1"):
-        early(1)
-
-    bias = small[:, ends[2] : ends[3]]
-    with jax.named_scope("k_out"):
-        for s in range(2):
-
-            @pl.when(tm > 0)
-            def _():
+            for s in range(2):
                 pltpu.make_async_copy(rbuf.at[s], rbuf.at[s], n_recv.at[s]).wait()
-
-            for k in (1, 0):
-                at_0, at_1, at_minus, at_inf = (prod[u, s] for u in range(4))
-                if k == 1:
-                    own = jnp.where(tm == 0, 2.0 * at_1 - at_0, at_1 - at_minus - at_inf)
-                else:
-                    own = jnp.where(tm == 0, 2.0 * at_1, at_0)
-                earlier = jnp.where(tm == 0, 0.0, rbuf[s, k].astype(F32))
-                value = (own + earlier + bias).astype(BF16)
-                for q, i in enumerate(row_sets[s]):
-                    out_ref[k, i] = value[q * cols : (q + 1) * cols]
+                for k in range(2):
+                    put(s, k, own[s, k] + rbuf[s, k].astype(F32))
 
     with jax.named_scope("l_tail"):
         pltpu.make_async_copy(stats.at[1:], stats.at[1:], s_send).wait()
 
-        @pl.when(hh < n_h - 1)
-        def _():
-            to_next.wait_send()
-
-        @pl.when(hh > 0)
-        def _():
-            to_last.wait_send()
+        for e in range(2):
+
+            @pl.when(edges[e][3])
+            def _():
+                pltpu.make_async_copy(edges[e][1], edges[e][1], h_send.at[e]).wait()
 
         @pl.when(tm < n_tm - 1)
         def _():
@@ -354,12 +378,13 @@
                 pltpu.VMEM((frames, rows, cols, channels), BF16),
                 pltpu.VMEM((1, 2 * channels + c_out), F32),
                 pltpu.VMEM((3, 3, 3, channels, c_out), BF16),
-                pltpu.VMEM((2, 3, 3, channels, c_out), BF16),
+                pltpu.VMEM((3, 3, 3, channels, c_out), BF16),
                 pltpu.VMEM((frames, cols, channels), BF16),
                 pltpu.VMEM((frames, cols, channels), BF16),
                 pltpu.VMEM((n_tm * n_h, 1, LANES), F32),
-                pltpu.VMEM((4, rows + 2, cols, channels), BF16),
-                pltpu.VMEM((4, 2, per_set, c_out), F32),
+                pltpu.VMEM((5, rows + 2, cols, channels), BF16),
+                pltpu.VMEM((4, per_set, c_out), F32),
+                pltpu.VMEM((2, 2, per_set, c_out), F32),
                 pltpu.VMEM((2, 2, per_set, c_out), BF16),
                 pltpu.VMEM((2, 2, per_set, c_out), BF16),
                 dma((frames, 2)),
@@ -368,7 +393,7 @@
                 dma,
                 dma,
                 dma((2,)),
-                dma((2,)),
+                dma((2, frames)),
                 dma,
                 dma((2,)),
             ],

time: 16.4 us -> 15.6 us (0.951)
  Pallas kernels: 15.5 us -> 14.7 us
    pallas_call x1, Pallas kernels: 15.5 us -> 14.7 us  [on_device(): pl.pallas_call(functools.partial(body, n_tm, n_h), out_shape=pltpu.VMEM((...]
where the time goes in v2:
time: 15.6 us; the launch traced here: 15.4 us
  Pallas kernels  14.7 us (94%)
  local copies, waits for them, and re-layouts  0.75 us (5%)
    pallas_call x1, Pallas kernels, on_device(): pl.pallas_call(functools.partial(body, n_tm, n_h), out_shape=pltpu.VMEM((...  14.7 us
    unnamed x1, local copies, waits for them, and re-layouts  0.75 us

profile of v2, /device:TPU:0, one launch (start us, length us, event | category | flops | bytes accessed | tf_op | source)
XLA Modules:
  0.0 15.4 jit_solution(17823008642048343901)
XLA Ops:
  0.0 14.7 %shard_map.55 = bf16[2,4,96,256]{3,2,1,0:T(8,128)(2,1)S(1)} custom-call(bf16[2,4,96,512]{3,2,1,0:T(8,128)(2,1)} %x_hbm.1, f32[1,512]{1,0:T(1,128)} %bitcast.3, f32[1,512]{1,0:T(1,128)} %bitcast.4, bf16[3,3,3,512,256]{4,3,2,1,0:T(8,128)(2,1)} %w_hbm.1, f32[1,256]{1,0:T(1,128)} %bitcast.5), custom_call_target="tpu_custom_call" | custom-call | tf_op jit(solution)/shard_map/pallas_call | solution.py:372
  14.7 0.7 %copy.7 = bf16[2,4,96,256]{3,2,1,0:T(8,128)(2,1)} copy(bf16[2,4,96,256]{3,2,1,0:T(8,128)(2,1)S(1)} %shard_map.55) | data formatting | bytes 786432

commit v3 on v2

--- a/solution.py
+++ b/solution.py
@@ -45,6 +45,7 @@
     bias_hbm,
     out_ref,
     x_vm,
+    x_wide,
     small,
     w_vm,
     u_vm,
@@ -57,13 +58,10 @@
     nbuf,
     rbuf,
     x_sem,
-    p_sem,
-    w_sem,
     s_send,
     s_recv,
     h_send,
     h_recv,
-    n_send,
     n_recv,
 ):
     frames, rows, cols, channels = x_vm.shape
@@ -93,10 +91,10 @@
     for d in range(1, count):
         pl.semaphore_signal(barrier, inc=1, device_id=peer(d), device_id_type=MESH)
     ends = (0, channels, 2 * channels, 2 * channels + c_out)
-    for i, ref in enumerate((gain_hbm, shift_hbm, bias_hbm)):
-        pltpu.make_async_copy(ref, small.at[:, ends[i] : ends[i + 1]], p_sem).start()
+    w_sems = (x_sem.at[0, 0], x_sem.at[0, 1], x_sem.at[1, 0])
+    p_sem = x_sem.at[1, 1]
     w_copies = [
-        pltpu.make_async_copy(w_hbm.at[:, :, c], w_vm.at[:, c], w_sem.at[c]) for c in range(3)
+        pltpu.make_async_copy(w_hbm.at[:, :, c], w_vm.at[:, c], w_sems[c]) for c in range(3)
     ]
     with jax.named_scope("a_sums"):
         sums = jnp.zeros((8, channels), F32)
@@ -107,9 +105,12 @@
             if p == 2 * frames - 1:
                 for copy in w_copies:
                     copy.start()
+                for i, ref in enumerate((gain_hbm, shift_hbm, bias_hbm)):
+                    pltpu.make_async_copy(ref, small.at[:, ends[i] : ends[i + 1]], p_sem).start()
             f = p // 2
             for r in range(p % 2 * half, p % 2 * half + half):
-                v = x_vm[f, r].astype(F32).reshape(cols // 8, 8, channels)
+                x_wide[f, r] = x_vm[f, r].astype(F32)
+                v = x_wide[f, r].reshape(cols // 8, 8, channels)
                 sums = sums + jnp.sum(v, axis=0)
                 squares = squares + jnp.sum(v * v, axis=0)
     with jax.named_scope("b_stat"):
@@ -183,6 +184,7 @@
     pltpu.make_async_copy(small, small, p_sem).wait()
     with jax.named_scope("e_shares"):
         pltpu.make_async_copy(stats.at[1:], stats.at[1:], s_recv).wait()
+        pltpu.make_async_copy(stats.at[1:], stats.at[1:], s_send).wait()
     total = jnp.sum(stats[...], axis=0)
     cells = n_tm * n_h * frames * rows * cols * per_group
     means = group_sums(jnp.where(own_lanes(parts), total, 0.0), parts) * (1.0 / cells)
@@ -212,15 +214,16 @@
 
     with jax.named_scope("f_act"):
         for r in range(rows):
-            lhs[F_1, r + 1] = activate(x_vm[1, r])
+            lhs[F_1, r + 1] = activate(x_wide[1, r])
         for r in range(rows):
-            place_first(r, activate(x_vm[0, r]))
-
-    def edge(e, f):
+            place_first(r, activate(x_wide[0, r]))
+
+    def arrived(e, f):
         @pl.when(edges[1 - e][3])
         def _():
             halo(e, f).wait_recv()
 
+    def edge(e, f):
         value = activate(edges[e][1][f])
         return jnp.where(edges[1 - e][3], value, jnp.zeros_like(value))
 
@@ -238,32 +241,34 @@
     def high_of(v):
         return jnp.where(not_last, pltpu.roll(v, m - 1, 0), 0.0)
 
+    def tap(u, weights, s, c, depth=slice(None)):
+        rows_of = [jnp.concatenate([lhs[u, i + b] for i in row_sets[s]], axis=0) for b in range(3)]
+        return jnp.dot(
+            jnp.concatenate(rows_of, axis=1)[:, depth],
+            weights[c].reshape(3 * channels, c_out)[depth],
+            preferred_element_type=F32,
+        )
+
+    def lows(u, weights, s, split=True):
+        halves = (slice(0, cut), slice(cut, None)) if split else (slice(None),)
+        return [tap(u, weights, s, 0, depth) for depth in halves]
+
     def taps(u, weights, s, split=False):
-        def tap(c, depth=slice(None)):
-            rows_of = [
-                jnp.concatenate([lhs[u, i + b] for i in row_sets[s]], axis=0) for b in range(3)
-            ]
-            return jnp.dot(
-                jnp.concatenate(rows_of, axis=1)[:, depth],
-                weights[c].reshape(3 * channels, c_out)[depth],
-                preferred_element_type=F32,
-            )
-
-        halves = (slice(0, cut), slice(cut, None)) if split else (slice(None),)
-        return tap(1), tap(2), *(tap(0, depth) for depth in halves)
+        high, low = tap(u, weights, s, 2), lows(u, weights, s, split)
+        return tap(u, weights, s, 1), high, *low
 
     def merge(parts_of):
         mid, high, *low = parts_of
-        value = mid + high_of(high)
+        value = high_of(high)
         for v in low:
             value = value + low_of(v)
-        return value
+        return value + mid
 
     def sends(s, k):
         return pltpu.make_async_remote_copy(
             src_ref=nbuf.at[s, k],
             dst_ref=rbuf.at[s, k],
-            send_sem=n_send,
+            send_sem=s_send,
             recv_sem=n_recv.at[s],
             device_id={"tm": lax.rem(tm + 1, n_tm)},
             device_id_type=MESH,
@@ -290,48 +295,60 @@
     w_half, w_half_minus, w_sum = (u_vm.at[u] for u in range(3))
 
     with jax.named_scope("g_inf0"):
-        p_inf = merge(taps(F_1, w_0, 0, split=False))
+        p_inf = merge(taps(F_1, w_0, 0))
         prod[0] = p_inf
         nbuf[0, 1] = p_inf.astype(BF16)
         ahead = taps(at_0, w_2, 0)
         send(0, 1)
         prod[1] = merge(ahead)
+        beside = tap(at_1, w_half, 0, 2)
+        prod[2] = high_of(beside)
 
     with jax.named_scope("h_halo1"):
+        for e in range(2):
+            arrived(e, 1)
+
+    with jax.named_scope("i_inf1"):
+        mid = tap(at_1, w_half, 0, 1)
         for e, row in ((0, -1), (1, rows)):
             lhs[F_1, row + 1] = edge(e, 1)
-
-    with jax.named_scope("i_inf1"):
-        nbuf[1, 1] = merge(taps(F_1, w_0, 1, split=False)).astype(BF16)
+        prod[2] = prod[2] + mid
+        nbuf[1, 1] = merge(taps(F_1, w_0, 1)).astype(BF16)
         for r in range(rows):
             lhs[LESS_TWICE, r + 1] = lhs[LESS, r + 1] - lhs[F_1, r + 1]
-        ahead = taps(at_1, w_half, 0)
         send(1, 1)
-        prod[2] = merge(ahead)
+        (low,) = lows(at_1, w_half, 0, False)
+        high = tap(at_minus, w_half_minus, 0, 2)
+        prod[2] = prod[2] + low_of(low)
 
     with jax.named_scope("i_rest0"):
-        prod[3] = merge(taps(at_minus, w_half_minus, 0))
+        (low,) = lows(at_minus, w_half_minus, 0, False)
+        prod[3] = merge((tap(at_minus, w_half_minus, 0, 1), high, low))
         p_inf, p_0, p_1, p_minus = (prod[i] for i in range(4))
         nbuf[0, 0] = (p_1 + p_minus - p_0 + first * p_inf).astype(BF16)
         finish(0, 0, jnp.where(tm == 0, 2.0 * p_1, p_0))
         finish(0, 1, jnp.where(tm == 0, 2.0 * p_1 - p_0, p_1 - p_minus - p_inf))
-        ahead = taps(F_1, w_1, 1)
+        ahead = (tap(F_1, w_1, 1, 2), *lows(F_1, w_1, 1, False))
         send(0, 0)
-        prod[1] = merge(ahead)
+        prod[1] = high_of(ahead[0]) + low_of(ahead[1])
 
     with jax.named_scope("h_halo0"):
+        for e in range(2):
+            arrived(e, 0)
+
+    with jax.named_scope("j_later1"):
+        mid = tap(F_1, w_1, 1, 1)
         for e, row in ((0, -1), (1, rows)):
             place_first(row, edge(e, 0))
-
-    with jax.named_scope("j_later1"):
-        prod[0] = merge(taps(F_0, w_0, 1, split=False))
+        prod[1] = prod[1] + mid
+        prod[0] = merge(taps(F_0, w_0, 1))
         nbuf[1, 0] = (prod[0] + prod[1]).astype(BF16)
         ahead = taps(at_0, w_2, 1)
         send(1, 0)
         prod[2] = merge(ahead)
 
     with jax.named_scope("j_rest1"):
-        prod[3] = merge(taps(at_1, w_sum, 1, split=True))
+        prod[3] = merge(taps(at_1, w_sum, 1))
         q_2, q_3, q_4, q_5 = (prod[i] for i in range(4))
         finish(1, 0, jnp.where(tm == 0, q_2 + q_5, q_4))
         finish(1, 1, q_5 - q_4 + jnp.where(tm == 0, q_2, -q_3))
@@ -345,8 +362,6 @@
                     put(s, k, own[s, k] + rbuf[s, k].astype(F32))
 
     with jax.named_scope("l_tail"):
-        pltpu.make_async_copy(stats.at[1:], stats.at[1:], s_send).wait()
-
         for e in range(2):
 
             @pl.when(edges[e][3])
@@ -355,7 +370,7 @@
 
         @pl.when(tm < n_tm - 1)
         def _():
-            pltpu.make_async_copy(nbuf, nbuf, n_send).wait()
+            pltpu.make_async_copy(nbuf, nbuf, s_send).wait()
 
 
 def solution(mesh):
@@ -376,6 +391,7 @@
             out_specs=vmem,
             scratch_shapes=[
                 pltpu.VMEM((frames, rows, cols, channels), BF16),
+                pltpu.VMEM((frames, rows, cols, channels), F32),
                 pltpu.VMEM((1, 2 * channels + c_out), F32),
                 pltpu.VMEM((3, 3, 3, channels, c_out), BF16),
                 pltpu.VMEM((3, 3, 3, channels, c_out), BF16),
@@ -389,12 +405,9 @@
                 pltpu.VMEM((2, 2, per_set, c_out), BF16),
                 dma((frames, 2)),
                 dma,
-                dma((3,)),
-                dma,
                 dma,
                 dma((2,)),
                 dma((2, frames)),
-                dma,
                 dma((2,)),
             ],
             compiler_params=pltpu.CompilerParams(

time: 15.6 us -> 15.3 us (0.981)
  Pallas kernels: 14.7 us -> 14.4 us
    pallas_call x1, Pallas kernels: 14.7 us -> 14.4 us  [on_device(): pl.pallas_call(functools.partial(body, n_tm, n_h), out_shape=pltpu.VMEM((...]
where the time goes in v3:
time: 15.3 us; the launch traced here: 15.1 us
  Pallas kernels  14.4 us (94%)
  local copies, waits for them, and re-layouts  0.75 us (5%)
    pallas_call x1, Pallas kernels, on_device(): pl.pallas_call(functools.partial(body, n_tm, n_h), out_shape=pltpu.VMEM((...  14.4 us
    unnamed x1, local copies, waits for them, and re-layouts  0.75 us

profile of v3, /device:TPU:0, one launch (start us, length us, event | category | flops | bytes accessed | tf_op | source)
XLA Modules:
  0.0 15.1 jit_solution(7982583906656954542)
XLA Ops:
  0.0 14.4 %shard_map.55 = bf16[2,4,96,256]{3,2,1,0:T(8,128)(2,1)S(1)} custom-call(bf16[2,4,96,512]{3,2,1,0:T(8,128)(2,1)} %x_hbm.1, f32[1,512]{1,0:T(1,128)} %bitcast.3, f32[1,512]{1,0:T(1,128)} %bitcast.4, bf16[3,3,3,512,256]{4,3,2,1,0:T(8,128)(2,1)} %w_hbm.1, f32[1,256]{1,0:T(1,128)} %bitcast.5), custom_call_target="tpu_custom_call" | custom-call | tf_op jit(solution)/shard_map/pallas_call | solution.py:387
  14.4 0.7 %copy.7 = bf16[2,4,96,256]{3,2,1,0:T(8,128)(2,1)} copy(bf16[2,4,96,256]{3,2,1,0:T(8,128)(2,1)S(1)} %shard_map.55) | data formatting | bytes 786432

commit v4 on v3

--- a/solution.py
+++ b/solution.py
@@ -330,9 +330,6 @@
         finish(0, 1, jnp.where(tm == 0, 2.0 * p_1 - p_0, p_1 - p_minus - p_inf))
         ahead = (tap(F_1, w_1, 1, 2), *lows(F_1, w_1, 1, False))
         send(0, 0)
-        prod[1] = high_of(ahead[0]) + low_of(ahead[1])
-
-    with jax.named_scope("h_halo0"):
         for e in range(2):
             arrived(e, 0)
 
@@ -340,18 +337,22 @@
         mid = tap(F_1, w_1, 1, 1)
         for e, row in ((0, -1), (1, rows)):
             place_first(row, edge(e, 0))
-        prod[1] = prod[1] + mid
+        prod[1] = merge((mid, *ahead))
         prod[0] = merge(taps(F_0, w_0, 1))
         nbuf[1, 0] = (prod[0] + prod[1]).astype(BF16)
-        ahead = taps(at_0, w_2, 1)
+        ahead = (tap(at_0, w_2, 1, 2), *lows(at_0, w_2, 1, False))
         send(1, 0)
-        prod[2] = merge(ahead)
 
     with jax.named_scope("j_rest1"):
-        prod[3] = merge(taps(at_1, w_sum, 1))
-        q_2, q_3, q_4, q_5 = (prod[i] for i in range(4))
-        finish(1, 0, jnp.where(tm == 0, q_2 + q_5, q_4))
-        finish(1, 1, q_5 - q_4 + jnp.where(tm == 0, q_2, -q_3))
+        q_2, q_3 = prod[0], prod[1]
+        sides_4 = high_of(ahead[0]) + low_of(ahead[1])
+        prod[2] = sides_4
+        sides_5 = high_of(tap(at_1, w_sum, 1, 2)) + low_of(*lows(at_1, w_sum, 1, False))
+        prod[3] = sides_5 - prod[2] + jnp.where(tm == 0, q_2, -q_3)
+        prod[2] = jnp.where(tm == 0, q_2 + sides_5, prod[2])
+        mid_5, mid_4 = tap(at_1, w_sum, 1, 1), tap(at_0, w_2, 1, 1)
+        finish(1, 0, prod[2] + jnp.where(tm == 0, mid_5, mid_4))
+        finish(1, 1, prod[3] + (mid_5 - mid_4))
 
     with jax.named_scope("k_out"):
         @pl.when(tm > 0)

time: 15.3 us -> 15.2 us (level)
  no operation moved by 1% of the time
where the time goes in v4:
time: 15.2 us; the launch traced here: 15.1 us
  Pallas kernels  14.3 us (94%)
  local copies, waits for them, and re-layouts  0.75 us (5%)
    pallas_call x1, Pallas kernels, on_device(): pl.pallas_call(functools.partial(body, n_tm, n_h), out_shape=pltpu.VMEM((...  14.3 us
    unnamed x1, local copies, waits for them, and re-layouts  0.75 us

profile of v4, /device:TPU:0, one launch (start us, length us, event | category | flops | bytes accessed | tf_op | source)
XLA Modules:
  0.0 15.1 jit_solution(17148461201017517814)
XLA Ops:
  0.0 14.3 %shard_map.55 = bf16[2,4,96,256]{3,2,1,0:T(8,128)(2,1)S(1)} custom-call(bf16[2,4,96,512]{3,2,1,0:T(8,128)(2,1)} %x_hbm.1, f32[1,512]{1,0:T(1,128)} %bitcast.3, f32[1,512]{1,0:T(1,128)} %bitcast.4, bf16[3,3,3,512,256]{4,3,2,1,0:T(8,128)(2,1)} %w_hbm.1, f32[1,256]{1,0:T(1,128)} %bitcast.5), custom_call_target="tpu_custom_call" | custom-call | tf_op jit(solution)/shard_map/pallas_call | solution.py:388
  14.3 0.7 %copy.7 = bf16[2,4,96,256]{3,2,1,0:T(8,128)(2,1)} copy(bf16[2,4,96,256]{3,2,1,0:T(8,128)(2,1)S(1)} %shard_map.55) | data formatting | bytes 786432
